TPU v7x, 512 devices: a whole 4x8x8 slice. The times are simulated.
512 devices in a mesh: gx: 8 (over z_lo, x), gy: 4 (over z_hi), gz: 16 (over y, core).
Axes of the slice: x: 4, y: 8, z: 8 (z_hi: 4, z_lo: 2; z = z_hi * 2 + z_lo), core: 2. Of those that a mesh axis runs over, the one named last changes fastest.
Arguments:
- vectors: float32 [3, 48, 24, 96, 128], P(None, 'gx', 'gy', 'gz'), may hold values from -6 to 6
- orient_flip: int32 [16, 8, 4608], P('gx', 'gy', 'gz'), may hold values from 0 to 1
- reluctivity: float32 [16, 8, 2048], P('gx', 'gy', 'gz'), may hold values from 0.05 to 0.5
- conductivity: float32 [16, 8, 2048], P('gx', 'gy', 'gz'), may hold values from 1 to 10
Outputs:
- out_x: float32 [48, 28, 112, 128], P('gx', 'gy', 'gz')
- out_y: float32 [56, 24, 112, 128], P('gx', 'gy', 'gz')
- out_z: float32 [56, 28, 96, 128], P('gx', 'gy', 'gz')
Inputs may be any that keep to these rules, and one draw needn't show every extreme that they name: `orient_flip`: 1 reverses the orientation of that degree of freedom in that element, 0 keeps it.
All inputs are finite; a program needn't handle non-finite values.
Results may differ from a plain program's by a relative error of at most 0.00007.
Values sent between devices are 32-bit elements; how exact they have to be, the bound alone decides.
A program may use at most 64 MiB of HBM per device.

v0:
```python
import jax
import jax.numpy as jnp
import numpy as np
from jax import lax
from jax.experimental import pallas as pl
from jax.experimental.pallas import tpu as pltpu
from jax.sharding import PartitionSpec as P

MESH = pl.DeviceIdType.MESH
AXES = ("gx", "gy", "gz")
LANES = 128
DOFS = 144
QPTS = 64
BASE = (0, 48, 96)
STRIDE = ((16, 4, 1), (12, 4, 1), (12, 3, 1))
EDGE_AXES = ((1, 2), (0, 2), (0, 1))
FACE_COMPS = ((1, 2), (0, 2), (0, 1))
SIGNS = ((-1, -1), (-1, 1), (1, -1), (1, 1))


def lagrange(points_at, evaluate_at):
    amount = len(points_at)
    values = np.ones((len(evaluate_at), amount))
    slopes = np.zeros((len(evaluate_at), amount))
    for which in range(amount):
        for column in range(amount):
            if column != which:
                factor = (evaluate_at - points_at[column]) / (points_at[which] - points_at[column])
                slopes[:, which] = slopes[:, which] * factor + values[:, which] / (
                    points_at[which] - points_at[column]
                )
                values[:, which] = values[:, which] * factor
    return (values, slopes)


def basis_tables():
    lobatto = np.array([0.0, (1 - 5 ** (-0.5)) / 2, (1 + 5 ** (-0.5)) / 2, 1.0])
    gauss_open = np.array([(1 - 0.6**0.5) / 2, 0.5, (1 + 0.6**0.5) / 2])
    inner_pt = (3.0 / 7 - 2.0 / 7 * (6.0 / 5) ** 0.5) ** 0.5
    outer_pt = (3.0 / 7 + 2.0 / 7 * (6.0 / 5) ** 0.5) ** 0.5
    inner_wt = (18 + 30**0.5) / 36
    outer_wt = (18 - 30**0.5) / 36
    quad_points = (1 + np.array([-outer_pt, -inner_pt, inner_pt, outer_pt])) / 2
    quad_weight = np.array([outer_wt, inner_wt, inner_wt, outer_wt]) / 2
    closed, slopes = lagrange(lobatto, quad_points)
    opened, unused_slopes = lagrange(gauss_open, quad_points)
    return (closed, slopes, opened, quad_weight)


CLOSED, SLOPES, OPENED, WEIGHT = basis_tables()
DERIV = SLOPES @ np.linalg.inv(CLOSED)


def apply(table, given, parity):
    rows, columns = table.shape
    half = columns // 2
    sums = [given[c] + given[columns - 1 - c] for c in range(half)]
    diffs = [given[c] - given[columns - 1 - c] for c in range(half)]
    result = [None] * rows
    for q in range((rows + 1) // 2):
        even = None
        for c in range(half):
            term = sums[c] * float((table[q, c] + table[q, columns - 1 - c]) / 2)
            even = term if even is None else even + term
        if columns % 2:
            even = even + given[half] * float(table[q, half])
        if 2 * q + 1 == rows:
            result[q] = even
            continue
        odd = None
        for c in range(half):
            term = diffs[c] * float((table[q, c] - table[q, columns - 1 - c]) / 2)
            odd = term if odd is None else odd + term
        result[q] = even + odd
        result[rows - 1 - q] = even - odd if parity > 0 else odd - even
    return result


def along_rows(table, plane, parity=1):
    columns = [apply(table, [row[c] for row in plane], parity) for c in range(len(plane[0]))]
    return [[column[q] for column in columns] for q in range(table.shape[0])]


def along_columns(table, plane, parity=1):
    return [apply(table, row, parity) for row in plane]


def combine(op, *planes):
    return [[op(*entries) for entries in zip(*rows)] for rows in zip(*planes)]


def plus(p, q):
    return combine(lambda s, t: s + t, p, q)


def minus(p, q):
    return combine(lambda s, t: s - t, p, q)


def times(p, q):
    return combine(lambda s, t: s * t, p, q)


def dof(comp, a, b, c):
    s = STRIDE[comp]
    return BASE[comp] + a * s[0] + b * s[1] + c * s[2]


def row_of(comp, a, b, c, element=0):
    return 8 * dof(comp, a, b, c) + element


def element(i, j, k):
    return 4 * k + 2 * i + j


def places(comp, axis):
    if comp == axis:
        return [(g, g // 3, g % 3) for g in range(6)]
    return [(g, 0, g) for g in range(4)] + [(g, 1, g - 3) for g in range(3, 7)]


def owners(comp, axis):
    last = 6 if comp == axis else 7
    return [(g, min(g // 3, 1), g - 3 * min(g // 3, 1)) for g in range(last)]


def prepare(flip, rel, con, flat, sign, mass, curl):
    for k in range(2):
        for i in range(2):
            at = pl.ds(4 * k + 2 * i, 2)
            flat[at, 0:DOFS] = 1.0 - 2.0 * flip[i][:, DOFS * k : DOFS * (k + 1)].astype(jnp.float32)
            flat[at, 256 : 256 + QPTS] = rel[i][:, QPTS * k : QPTS * (k + 1)]
            flat[at, 384 : 384 + QPTS] = con[i][:, QPTS * k : QPTS * (k + 1)]
    whole = flat[:, 0:DOFS]
    for d in range(DOFS):
        sign[d] = jnp.broadcast_to(whole[:, d : d + 1], (8, LANES))
    rel_all = flat[:, 256 : 256 + QPTS]
    con_all = flat[:, 384 : 384 + QPTS]
    for q in range(QPTS):
        weight = float(WEIGHT[q // 16] * WEIGHT[q // 4 % 4] * WEIGHT[q % 4])
        curl[q] = jnp.broadcast_to(rel_all[:, q : q + 1], (8, LANES)) * weight
        mass[q] = jnp.broadcast_to(con_all[:, q : q + 1], (8, LANES)) * weight


def compute(dofs, sign, mass, curl, temp, u_x, u_y, c_x, c_y, c_z):
    def load(d):
        return dofs[pl.ds(pl.multiple_of(8 * d, 8), 8), :] * sign[d]

    def store(d, value):
        dofs[pl.ds(pl.multiple_of(8 * d, 8), 8), :] = value * sign[d]

    def quad(x, y, z):
        return 16 * x + 4 * y + z

    four = range(4)

    def planes(ref, at):
        return [[ref[at(p, q)] for q in four] for p in four]

    def put(ref, at, plane):
        for p in four:
            for q in four:
                ref[at(p, q)] = plane[p][q]

    @pl.loop(0, 4)
    def _(b):
        for c in four:
            values = apply(OPENED, [load(dof(0, a, b, c)) for a in range(3)], 1)
            for q in four:
                temp[quad(q, b, c)] = values[q]

    @pl.loop(0, 4)
    def _(x):
        at = lambda y, z: quad(x, y, z)
        u = along_columns(CLOSED, along_rows(CLOSED, planes(temp, at)))
        put(u_x, at, u)
        put(c_z, at, along_rows(-DERIV, u, -1))
        put(c_y, at, along_columns(DERIV, u, -1))

    @pl.loop(0, 4)
    def _(a):
        values = [[load(dof(1, a, b, c)) for c in four] for b in range(3)]
        put(temp, lambda y, z: quad(a, y, z), along_columns(CLOSED, along_rows(OPENED, values)))

    @pl.loop(0, 4)
    def _(y):
        at = lambda x, z: quad(x, y, z)
        u = along_rows(CLOSED, planes(temp, at))
        put(u_y, at, u)
        put(c_z, at, plus(planes(c_z, at), along_rows(DERIV, u, -1)))
        put(c_x, at, along_columns(-DERIV, u, -1))

    @pl.loop(0, 4)
    def _(a):
        values = [[load(dof(2, a, b, c)) for c in range(3)] for b in four]
        put(temp, lambda y, z: quad(a, y, z), along_rows(CLOSED, along_columns(OPENED, values)))

    @pl.loop(0, 4)
    def _(z):
        at = lambda x, y: quad(x, y, z)
        u = along_rows(CLOSED, planes(temp, at))
        scale = planes(curl, at)
        w_y = times(scale, minus(planes(c_y, at), along_rows(DERIV, u, -1)))
        w_x = times(scale, plus(planes(c_x, at), along_columns(DERIV, u, -1)))
        put(c_y, at, w_y)
        put(c_x, at, w_x)
        v = times(planes(mass, at), u)
        v = plus(v, along_columns(DERIV.T, w_x, -1))
        v = minus(v, along_rows(DERIV.T, w_y, -1))
        put(temp, at, along_rows(CLOSED.T, v))

    @pl.loop(0, 4)
    def _(a):
        values = along_rows(CLOSED.T, planes(temp, lambda y, z: quad(a, y, z)))
        values = along_columns(OPENED.T, values)
        for b in four:
            for c in range(3):
                store(dof(2, a, b, c), values[b][c])

    @pl.loop(0, 4)
    def _(y):
        at = lambda x, z: quad(x, y, z)
        w_z = times(planes(curl, at), planes(c_z, at))
        put(c_z, at, w_z)
        v = times(planes(mass, at), planes(u_y, at))
        v = plus(v, along_rows(DERIV.T, w_z, -1))
        v = minus(v, along_columns(DERIV.T, planes(c_x, at), -1))
        put(temp, at, along_rows(CLOSED.T, v))

    @pl.loop(0, 4)
    def _(a):
        values = along_columns(CLOSED.T, planes(temp, lambda y, z: quad(a, y, z)))
        values = along_rows(OPENED.T, values)
        for b in range(3):
            for c in four:
                store(dof(1, a, b, c), values[b][c])

    @pl.loop(0, 4)
    def _(x):
        at = lambda y, z: quad(x, y, z)
        v = times(planes(mass, at), planes(u_x, at))
        v = plus(v, along_columns(DERIV.T, planes(c_y, at), -1))
        v = minus(v, along_rows(DERIV.T, planes(c_z, at), -1))
        put(temp, at, along_rows(CLOSED.T, along_columns(CLOSED.T, v)))

    @pl.loop(0, 4)
    def _(b):
        for c in four:
            values = apply(OPENED.T, [temp[quad(q, b, c)] for q in four], 1)
            for a in range(3):
                store(dof(0, a, b, c), values[a])


def join_elements(dofs):
    rows = lax.broadcasted_iota(jnp.int32, (8, LANES), 0)
    for axis, step in ((0, 2), (1, 1), (2, 4)):
        upper = (rows // step) % 2 == 1
        for comp in range(3):
            if comp == axis:
                continue
            sizes = [3 if comp == other else 4 for other in range(3)]
            sizes[axis] = 1
            for a in range(sizes[0]):
                for b in range(sizes[1]):
                    for c in range(sizes[2]):
                        low = [a, b, c]
                        high = [a, b, c]
                        high[axis] = 3
                        to = pl.ds(row_of(comp, *low), 8)
                        moved = pltpu.roll(dofs[pl.ds(row_of(comp, *high), 8), :], step, 0)
                        dofs[to, :] = dofs[to, :] + jnp.where(upper, moved, 0.0)


def scatter_own(vec, dofs):
    for comp in range(3):
        for x, i, a in places(comp, 0):
            for y, j, b in places(comp, 1):
                if x == 6 or y == 6:
                    continue
                for k in range(2):
                    count = 4 if comp != 2 and k == 0 else 3
                    at = row_of(comp, a, b, 0, element(i, j, k))
                    dofs[pl.ds(at, count, 8), :] = vec[comp, x, y, pl.ds(3 * k, count), :]


def scatter_halo(dofs, r_x, r_y, r_z, r_e):
    def line(comp, i, a, j, b, source):
        for k in range(2):
            count = 4 if comp != 2 and k == 0 else 3
            at = row_of(comp, a, b, 0, element(i, j, k))
            dofs[pl.ds(at, count, 8), :] = source(pl.ds(3 * k, count))

    for comp in (1, 2):
        for y, j, b in places(comp, 1):
            if y < 6:
                line(comp, 1, 3, j, b, lambda z: r_x[comp - 1, y, z, :])
    for comp in (0, 2):
        for x, i, a in places(comp, 0):
            if x < 6:
                line(comp, i, a, 1, 3, lambda z: r_y[comp // 2, x, z, :])
    line(2, 1, 3, 1, 3, lambda z: r_e[2, z, :])
    for x, i, a in places(0, 0):
        for j in range(2):
            count = 4 - j
            at = row_of(0, a, 0, 3, element(i, j, 1))
            dofs[pl.ds(at, count, 32), :] = r_z[0, x, pl.ds(3 * j, count), :]
    for x, i, a in places(1, 0):
        if x < 6:
            for j in range(2):
                at = row_of(1, a, 0, 3, element(i, j, 1))
                dofs[pl.ds(at, 3, 32), :] = r_z[1, x, pl.ds(3 * j, 3), :]
    for i in range(2):
        at = row_of(0, 0, 3, 3, element(i, 1, 1))
        dofs[pl.ds(at, 3, 128), :] = r_e[0, pl.ds(3 * i, 3), :]
    for j in range(2):
        at = row_of(1, 3, 0, 3, element(1, j, 1))
        dofs[pl.ds(at, 3, 32), :] = r_e[1, pl.ds(3 * j, 3), :]


def to_grid(dofs, outs):
    for comp in range(3):
        for x, i, a in owners(comp, 0):
            for y, j, b in owners(comp, 1):
                for k in range(2):
                    count = 3 + k * (comp != 2)
                    at = row_of(comp, a, b, 0, element(i, j, k))
                    outs[comp][x, y, pl.ds(3 * k, count), :] = dofs[pl.ds(at, count, 8), :]


def pack_shared(dofs, pack_x, pack_y, edges):
    for side in range(2):
        c = 3 * side
        for x, i, a in owners(0, 0):
            for j in range(2):
                at = row_of(0, a, 0, c, element(i, j, side))
                pack_x[side, x, pl.ds(3 * j, 3 + j), :] = dofs[pl.ds(at, 3 + j, 32), :]
        for x, i, a in owners(1, 0):
            for j in range(2):
                at = row_of(1, a, 0, c, element(i, j, side))
                pack_y[side, x, pl.ds(3 * j, 3), :] = dofs[pl.ds(at, 3, 32), :]
    for n, (first, second) in enumerate(SIGNS):
        p, q = first > 0, second > 0
        for i in range(2):
            at = row_of(0, 0, 3 * p, 3 * q, element(i, int(p), int(q)))
            edges[0, n, pl.ds(3 * i, 3), :] = dofs[pl.ds(at, 3, 128), :]
        for j in range(2):
            at = row_of(1, 3 * p, 0, 3 * q, element(int(p), j, int(q)))
            edges[1, n, pl.ds(3 * j, 3), :] = dofs[pl.ds(at, 3, 32), :]


def add_shared(outs, f_x, f_y, f_zx, f_zy, f_e):
    out_x, out_y, out_z = outs
    for side in range(2):
        at = 6 * side
        out_y[at] = out_y[at] + f_x[0][side]
        out_z[at] = out_z[at] + f_x[1][side]
        for x in range(6):
            out_x[x, at] = out_x[x, at] + f_y[0][side, x]
        for x in range(7):
            out_z[x, at] = out_z[x, at] + f_y[1][side, x]
        z = pl.ds(at, 1)
        for x in range(6):
            for y in range(7):
                out_x[x, y, z, :] = out_x[x, y, z, :] + f_zx[side, x, pl.ds(y, 1), :]
        for x in range(7):
            for y in range(6):
                out_y[x, y, z, :] = out_y[x, y, z, :] + f_zy[side, x, pl.ds(y, 1), :]
    for n, (first, second) in enumerate(SIGNS):
        p, q = 6 * (first > 0), 6 * (second > 0)
        for x in range(6):
            z = pl.ds(q, 1)
            out_x[x, p, z, :] = out_x[x, p, z, :] + f_e[0, n, pl.ds(x, 1), :]
        for y in range(6):
            z = pl.ds(q, 1)
            out_y[p, y, z, :] = out_y[p, y, z, :] + f_e[1, n, pl.ds(y, 1), :]
        out_z[p, q] = out_z[p, q] + f_e[2, n]


def kernel(
    sizes,
    vec_hbm,
    flip_hbm,
    rel_hbm,
    con_hbm,
    out_x,
    out_y,
    out_z,
    vec,
    flip,
    rel,
    con,
    flat,
    sign,
    mass,
    curl,
    dofs,
    temp,
    u_x,
    u_y,
    c_x,
    c_y,
    c_z,
    s_z,
    s_e,
    r_x,
    r_y,
    r_z,
    r_e,
    pack_x,
    pack_y,
    edges,
    f_xy,
    f_xz,
    f_yx,
    f_yz,
    f_zx,
    f_zy,
    f_e,
    load_sem,
    send_sem,
    recv_sem,
):
    me = [lax.axis_index(axis) for axis in AXES]

    def neighbour(*steps):
        return tuple(lax.rem(me[n] + steps[n] + sizes[n], sizes[n]) for n in range(3))

    loads = [
        pltpu.make_async_copy(source, target, load_sem.at[n])
        for n, (source, target) in enumerate(
            ((vec_hbm, vec), (flip_hbm, flip), (rel_hbm, rel), (con_hbm, con))
        )
    ]
    for copy in loads:
        copy.start()

    barrier = pltpu.get_barrier_semaphore()
    around = []
    for axis in range(3):
        for step in (-1, 1):
            around.append([step * (axis == n) for n in range(3)])
    for pair in EDGE_AXES:
        for first, second in SIGNS:
            around.append([first * (n == pair[0]) + second * (n == pair[1]) for n in range(3)])
    for steps in around:
        pl.semaphore_signal(barrier, inc=1, device_id=neighbour(*steps), device_id_type=MESH)

    copies = []

    def send(source, target, *steps):
        n = len(copies)
        copy = pltpu.make_async_remote_copy(
            src_ref=source,
            dst_ref=target,
            send_sem=send_sem.at[n],
            recv_sem=recv_sem.at[n],
            device_id=neighbour(*steps),
            device_id_type=MESH,
        )
        copy.start()
        copies.append(copy)

    loads[0].wait()
    for comp in range(2):
        for x in range(6):
            for y in range(6):
                s_z[comp, x, pl.ds(y, 1), :] = vec[comp, x, y, pl.ds(0, 1), :]
    for n in range(6):
        s_e[0, pl.ds(n, 1), :] = vec[0, n, 0, pl.ds(0, 1), :]
        s_e[1, pl.ds(n, 1), :] = vec[1, 0, n, pl.ds(0, 1), :]
    pl.semaphore_wait(barrier, len(around))
    send(vec.at[0, :, 0], r_y.at[0], 0, -1, 0)
    send(vec.at[2, :, 0], r_y.at[1], 0, -1, 0)
    send(vec.at[pl.ds(1, 2), 0], r_x, -1, 0, 0)
    send(s_z, r_z, 0, 0, -1)
    send(s_e.at[0], r_e.at[0], 0, -1, -1)
    send(s_e.at[1], r_e.at[1], -1, 0, -1)
    send(vec.at[2, 0, 0], r_e.at[2], -1, -1, 0)

    scatter_own(vec, dofs)
    for copy in loads[1:]:
        copy.wait()
    prepare(flip, rel, con, flat, sign, mass, curl)
    for copy in copies:
        copy.wait_recv()
    scatter_halo(dofs, r_x, r_y, r_z, r_e)
    compute(dofs, sign, mass, curl, temp, u_x, u_y, c_x, c_y, c_z)
    join_elements(dofs)
    outs = (out_x, out_y, out_z)
    to_grid(dofs, outs)
    pack_shared(dofs, pack_x, pack_y, edges)

    halo = len(copies)
    for side, step in enumerate((-1, 1)):
        at, other = 6 * side, 1 - side
        send(out_x.at[:, at], f_yx.at[other], 0, step, 0)
        send(out_z.at[:, at], f_yz.at[other], 0, step, 0)
        send(out_y.at[at], f_xy.at[other], step, 0, 0)
        send(out_z.at[at], f_xz.at[other], step, 0, 0)
        send(pack_x.at[side], f_zx.at[other], 0, 0, step)
        send(pack_y.at[side], f_zy.at[other], 0, 0, step)
    for n, (first, second) in enumerate(SIGNS):
        p, q = 6 * (first > 0), 6 * (second > 0)
        send(edges.at[0, n], f_e.at[0, 3 - n], 0, first, second)
        send(edges.at[1, n], f_e.at[1, 3 - n], first, 0, second)
        send(out_z.at[p, q], f_e.at[2, 3 - n], first, second, 0)
    for copy in copies[halo:]:
        copy.wait_recv()
    for copy in copies:
        copy.wait_send()
    add_shared(outs, (f_xy, f_xz), (f_yx, f_yz), f_zx, f_zy, f_e)


def on_device(sizes, vectors, orient_flip, reluctivity, conductivity):
    f32 = jnp.float32
    regs = lambda n: pltpu.VMEM((n, 8, LANES), f32)
    grid = ((6, 7, 7, LANES), (7, 6, 7, LANES), (7, 7, 6, LANES))
    return pl.pallas_call(
        lambda *refs: kernel(sizes, *refs),
        out_shape=[jax.ShapeDtypeStruct(shape, f32) for shape in grid],
        in_specs=[pl.BlockSpec(memory_space=pl.ANY)] * 4,
        out_specs=[pl.BlockSpec(memory_space=pltpu.VMEM)] * 3,
        scratch_shapes=[
            pltpu.VMEM((3, 6, 6, 6, LANES), f32),
            pltpu.VMEM(orient_flip.shape, jnp.int32),
            pltpu.VMEM(reluctivity.shape, f32),
            pltpu.VMEM(conductivity.shape, f32),
            pltpu.VMEM((8, 512), f32),
            regs(DOFS),
            regs(QPTS),
            regs(QPTS),
            pltpu.VMEM((8 * DOFS, LANES), f32),
            regs(QPTS),
            regs(QPTS),
            regs(QPTS),
            regs(QPTS),
            regs(QPTS),
            regs(QPTS),
            pltpu.VMEM((2, 6, 6, LANES), f32),
            pltpu.VMEM((2, 6, LANES), f32),
            pltpu.VMEM((2, 6, 6, LANES), f32),
            pltpu.VMEM((2, 6, 6, LANES), f32),
            pltpu.VMEM((2, 6, 6, LANES), f32),
            pltpu.VMEM((3, 6, LANES), f32),
            pltpu.VMEM((2, 6, 7, LANES), f32),
            pltpu.VMEM((2, 7, 6, LANES), f32),
            pltpu.VMEM((2, 4, 6, LANES), f32),
            pltpu.VMEM((2, 6, 7, LANES), f32),
            pltpu.VMEM((2, 7, 6, LANES), f32),
            pltpu.VMEM((2, 6, 7, LANES), f32),
            pltpu.VMEM((2, 7, 6, LANES), f32),
            pltpu.VMEM((2, 6, 7, LANES), f32),
            pltpu.VMEM((2, 7, 6, LANES), f32),
            pltpu.VMEM((3, 4, 6, LANES), f32),
            pltpu.SemaphoreType.DMA((4,)),
            pltpu.SemaphoreType.DMA((31,)),
            pltpu.SemaphoreType.DMA((31,)),
        ],
        compiler_params=pltpu.CompilerParams(collective_id=0, has_side_effects=True),
        name="curlcurl",
    )(vectors, orient_flip, reluctivity, conductivity)


def solution(mesh):
    sizes = tuple(mesh.shape[axis] for axis in AXES)
    return jax.shard_map(
        lambda *args: tuple(on_device(sizes, *args)),
        mesh=mesh,
        in_specs=(
            P(None, "gx", "gy", "gz", None),
            P("gx", "gy", "gz"),
            P("gx", "gy", "gz"),
            P("gx", "gy", "gz"),
        ),
        out_specs=(P("gx", "gy", "gz", None), P("gx", "gy", "gz", None), P("gx", "gy", "gz", None)),
        check_vma=False,
    )
```

profile of v0, /device:TPU:24, one launch (start us, length us, event | category | flops | bytes accessed | tf_op | source)
XLA Modules:
  0.0 32.8 jit_solution(15091461840432039029)
XLA Ops:
  0.6 28.8 %curlcurl.1 = (f32[6,7,7,128]{3,2,1,0:T(8,128)}, f32[7,6,7,128]{3,2,1,0:T(8,128)}, f32[7,7,6,128]{3,2,1,0:T(8,128)}) custom-call(f32[3,6,6,6,128]{4,3,2,1,0:T(8,128)} %refs_0_.1, s32[2,2,288]{2,1,0:T(2,128)} %refs_1_.1, f32[2,2,128]{2,1,0:T(2,128)} %refs_2_.1, f32[2,2,128]{2,1,0:T(2,128)} %refs_3_.1), custom_call_target="tpu_custom_call" | custom-call | tf_op jit(solution)/shard_map/curlcurl/pallas_call | solution.py:519
  29.5 0.0 copy-start.1
  29.5 1.7 %copy.7 = f32[7,7,6,128]{3,1,2,0:T(8,128)} copy(f32[7,7,6,128]{3,2,1,0:T(8,128)} %get-tuple-element.5) | data formatting | bytes 301056 | tf_op jit(solution)/shard_map/curlcurl/pallas_call | solution.py:519
  31.1 0.0 copy-done.1
  31.1 0.0 copy-start
  31.1 0.7 %copy.10 = f32[6,7,7,128]{3,2,1,0:T(8,128)} copy(f32[6,7,7,128]{3,2,1,0:T(8,128)S(1)} %copy-done.1) | data formatting | bytes 301056
  31.8 0.3 copy-done
  32.1 0.7 %copy.11 = f32[7,6,7,128]{3,2,1,0:T(8,128)} copy(f32[7,6,7,128]{3,2,1,0:T(8,128)S(1)} %copy-done) | data formatting | bytes 301056
Async XLA Ops:
  29.5 1.7 %copy-start.1 = (f32[6,7,7,128]{3,2,1,0:T(8,128)S(1)}, f32[6,7,7,128]{3,2,1,0:T(8,128)}, u32[]{:S(2)}) copy-start(f32[6,7,7,128]{3,2,1,0:T(8,128)} %get-tuple-element.9) | copy-start | bytes 451588
  31.1 1.0 %copy-start = (f32[7,6,7,128]{3,2,1,0:T(8,128)S(1)}, f32[7,6,7,128]{3,2,1,0:T(8,128)}, u32[]{:S(2)}) copy-start(f32[7,6,7,128]{3,2,1,0:T(8,128)} %get-tuple-element.10) | copy-start | bytes 451588
where the time goes:
time: 33 us; the launch traced here: 32.8 us
  Pallas kernels  28.8 us (87%)
  local copies, waits for them, and re-layouts  3.32 us (10%)
  between operations  0.65 us (2%)
    pallas_call x1, Pallas kernels, on_device(): pl.pallas_call(lambda *refs: kernel(sizes, *refs), out_shape=[jax.ShapeDt...  28.8 us
    pallas_call x1, local copies, waits for them, and re-layouts, on_device(): pl.pallas_call(lambda *refs: kernel(sizes, *refs), out_shape=[jax.ShapeDt...  1.67 us
    unnamed x6, local copies, waits for them, and re-layouts  1.65 us

commit v1 on v0

v1 whole, which is shorter than its diff:
```python
import jax
import jax.numpy as jnp
import numpy as np
from jax import lax
from jax.experimental import pallas as pl
from jax.experimental.pallas import tpu as pltpu
from jax.sharding import PartitionSpec as P

MESH = pl.DeviceIdType.MESH
AXES = ("gx", "gy", "gz")
LANES = 128
DOFS = 144
QPTS = 64
BASE = (0, 48, 96)
STRIDE = ((16, 4, 1), (12, 4, 1), (12, 3, 1))
EDGE_AXES = ((1, 2), (0, 2), (0, 1))
SIGNS = ((-1, -1), (-1, 1), (1, -1), (1, 1))


def lagrange(points_at, evaluate_at):
    amount = len(points_at)
    values = np.ones((len(evaluate_at), amount))
    slopes = np.zeros((len(evaluate_at), amount))
    for which in range(amount):
        for column in range(amount):
            if column != which:
                factor = (evaluate_at - points_at[column]) / (points_at[which] - points_at[column])
                slopes[:, which] = slopes[:, which] * factor + values[:, which] / (
                    points_at[which] - points_at[column]
                )
                values[:, which] = values[:, which] * factor
    return (values, slopes)


def basis_tables():
    lobatto = np.array([0.0, (1 - 5 ** (-0.5)) / 2, (1 + 5 ** (-0.5)) / 2, 1.0])
    gauss_open = np.array([(1 - 0.6**0.5) / 2, 0.5, (1 + 0.6**0.5) / 2])
    inner_pt = (3.0 / 7 - 2.0 / 7 * (6.0 / 5) ** 0.5) ** 0.5
    outer_pt = (3.0 / 7 + 2.0 / 7 * (6.0 / 5) ** 0.5) ** 0.5
    inner_wt = (18 + 30**0.5) / 36
    outer_wt = (18 - 30**0.5) / 36
    quad_points = (1 + np.array([-outer_pt, -inner_pt, inner_pt, outer_pt])) / 2
    quad_weight = np.array([outer_wt, inner_wt, inner_wt, outer_wt]) / 2
    closed, slopes = lagrange(lobatto, quad_points)
    opened, unused_slopes = lagrange(gauss_open, quad_points)
    return (closed, slopes, opened, quad_weight)


CLOSED, SLOPES, OPENED, WEIGHT = basis_tables()
DERIV = SLOPES @ np.linalg.inv(CLOSED)


def apply(table, given, parity):
    rows, columns = table.shape
    half = columns // 2
    sums = [given[c] + given[columns - 1 - c] for c in range(half)]
    diffs = [given[c] - given[columns - 1 - c] for c in range(half)]
    result = [None] * rows
    for q in range((rows + 1) // 2):
        even = None
        for c in range(half):
            term = sums[c] * float((table[q, c] + table[q, columns - 1 - c]) / 2)
            even = term if even is None else even + term
        if columns % 2:
            even = even + given[half] * float(table[q, half])
        if 2 * q + 1 == rows:
            result[q] = even
            continue
        odd = None
        for c in range(half):
            term = diffs[c] * float((table[q, c] - table[q, columns - 1 - c]) / 2)
            odd = term if odd is None else odd + term
        result[q] = even + odd
        result[rows - 1 - q] = even - odd if parity > 0 else odd - even
    return result


def along_rows(table, plane, parity=1):
    columns = [apply(table, [row[c] for row in plane], parity) for c in range(len(plane[0]))]
    return [[column[q] for column in columns] for q in range(table.shape[0])]


def along_columns(table, plane, parity=1):
    return [apply(table, row, parity) for row in plane]


def combine(op, *planes):
    return [[op(*entries) for entries in zip(*rows)] for rows in zip(*planes)]


def plus(p, q):
    return combine(lambda s, t: s + t, p, q)


def minus(p, q):
    return combine(lambda s, t: s - t, p, q)


def times(p, q):
    return combine(lambda s, t: s * t, p, q)


def dof(comp, a, b, c):
    s = STRIDE[comp]
    return BASE[comp] + a * s[0] + b * s[1] + c * s[2]


def row_of(comp, a, b, c, element=0):
    return 8 * dof(comp, a, b, c) + element


def element(i, j, k):
    return 4 * k + 2 * i + j


def places(comp, axis):
    if comp == axis:
        return [(g, g // 3, g % 3) for g in range(6)]
    return [(g, 0, g) for g in range(4)] + [(g, 1, g - 3) for g in range(3, 7)]


def owners(comp, axis):
    last = 6 if comp == axis else 7
    return [(g, min(g // 3, 1), g - 3 * min(g // 3, 1)) for g in range(last)]


def prepare(flip, rel, con, flat, sign, mass, curl):
    for k in range(2):
        for i in range(2):
            at = pl.ds(4 * k + 2 * i, 2)
            flat[at, 0:DOFS] = 1.0 - 2.0 * flip[i][:, DOFS * k : DOFS * (k + 1)].astype(jnp.float32)
            flat[at, 256 : 256 + QPTS] = rel[i][:, QPTS * k : QPTS * (k + 1)]
            flat[at, 384 : 384 + QPTS] = con[i][:, QPTS * k : QPTS * (k + 1)]
    whole = flat[:, 0:DOFS]
    for d in range(DOFS):
        sign[d] = jnp.broadcast_to(whole[:, d : d + 1], (8, LANES))
    rel_all = flat[:, 256 : 256 + QPTS]
    con_all = flat[:, 384 : 384 + QPTS]
    for q in range(QPTS):
        weight = float(WEIGHT[q // 16] * WEIGHT[q // 4 % 4] * WEIGHT[q % 4])
        curl[q] = jnp.broadcast_to(rel_all[:, q : q + 1], (8, LANES)) * weight
        mass[q] = jnp.broadcast_to(con_all[:, q : q + 1], (8, LANES)) * weight


def quad(x, y, z):
    return 16 * x + 4 * y + z


def planes(ref, at):
    return [[ref[at(p, q)] for q in range(4)] for p in range(4)]


def put(ref, at, plane):
    for p, row in enumerate(plane):
        for q, value in enumerate(row):
            ref[at(p, q)] = value


def load_plane(dofs, sign, rows):
    return [
        [dofs[pl.ds(pl.multiple_of(8 * d, 8), 8), :] * sign[d] for d in row] for row in rows
    ]


def store_plane(dofs, sign, rows, plane):
    for row, values in zip(rows, plane):
        for d, value in zip(row, values):
            dofs[pl.ds(pl.multiple_of(8 * d, 8), 8), :] = value * sign[d]


def rows_fixed_b(comp, b):
    return [[dof(comp, a, b, c) for c in range(4 - (comp == 2))] for a in range(4 - (comp == 0))]


def rows_fixed_a(comp, a):
    return [[dof(comp, a, b, c) for c in range(4)] for b in range(3)]


def forward_y(dofs, sign, temp, u_y, c_x, c_z):
    @pl.loop(0, 4)
    def _(a):
        values = along_rows(OPENED, load_plane(dofs, sign, rows_fixed_a(1, a)))
        put(temp, lambda y, z: quad(a, y, z), along_columns(CLOSED, values))

    @pl.loop(0, 4)
    def _(y):
        at = lambda x, z: quad(x, y, z)
        u = along_rows(CLOSED, planes(temp, at))
        put(u_y, at, u)
        put(c_z, at, along_rows(DERIV, u, -1))
        put(c_x, at, along_columns(-DERIV, u, -1))


def start_x(dofs, sign, temp, b):
    values = along_rows(OPENED, load_plane(dofs, sign, rows_fixed_b(0, b)))
    put(temp, lambda x, z: quad(x, b, z), along_columns(CLOSED, values))


def start_z(dofs, sign, temp, b):
    values = along_columns(OPENED, load_plane(dofs, sign, rows_fixed_b(2, b)))
    put(temp, lambda x, z: quad(x, b, z), along_rows(CLOSED, values))


def forward_x(temp, curl, u_x, c_y, c_z):
    @pl.loop(0, 4)
    def _(x):
        at = lambda y, z: quad(x, y, z)
        u = along_rows(CLOSED, planes(temp, at))
        put(u_x, at, u)
        w_z = minus(planes(c_z, at), along_rows(DERIV, u, -1))
        put(c_z, at, times(planes(curl, at), w_z))
        put(c_y, at, along_columns(DERIV, u, -1))


def turn_z(temp, mass, curl, c_x, c_y):
    @pl.loop(0, 4)
    def _(z):
        at = lambda x, y: quad(x, y, z)
        u = along_columns(CLOSED, planes(temp, at))
        scale = planes(curl, at)
        w_y = times(scale, minus(planes(c_y, at), along_rows(DERIV, u, -1)))
        w_x = times(scale, plus(planes(c_x, at), along_columns(DERIV, u, -1)))
        put(c_y, at, w_y)
        put(c_x, at, w_x)
        v = times(planes(mass, at), u)
        v = plus(v, along_columns(DERIV.T, w_x, -1))
        v = minus(v, along_rows(DERIV.T, w_y, -1))
        put(temp, at, along_columns(CLOSED.T, v))


def finish_z(dofs, sign, temp):
    @pl.loop(0, 4)
    def _(b):
        values = along_rows(CLOSED.T, planes(temp, lambda x, z: quad(x, b, z)))
        store_plane(dofs, sign, rows_fixed_b(2, b), along_columns(OPENED.T, values))


def backward_x(dofs, sign, mass, temp, u_x, c_y, c_z):
    @pl.loop(0, 4)
    def _(x):
        at = lambda y, z: quad(x, y, z)
        v = times(planes(mass, at), planes(u_x, at))
        v = plus(v, along_columns(DERIV.T, planes(c_y, at), -1))
        v = minus(v, along_rows(DERIV.T, planes(c_z, at), -1))
        put(temp, at, along_rows(CLOSED.T, v))

    @pl.loop(0, 4)
    def _(b):
        values = along_columns(CLOSED.T, planes(temp, lambda x, z: quad(x, b, z)))
        store_plane(dofs, sign, rows_fixed_b(0, b), along_rows(OPENED.T, values))


def backward_y(dofs, sign, mass, temp, u_y, c_x, c_z):
    @pl.loop(0, 4)
    def _(y):
        at = lambda x, z: quad(x, y, z)
        v = times(planes(mass, at), planes(u_y, at))
        v = plus(v, along_rows(DERIV.T, planes(c_z, at), -1))
        v = minus(v, along_columns(DERIV.T, planes(c_x, at), -1))
        put(temp, at, along_rows(CLOSED.T, v))

    @pl.loop(0, 4)
    def _(a):
        values = along_columns(CLOSED.T, planes(temp, lambda y, z: quad(a, y, z)))
        store_plane(dofs, sign, rows_fixed_a(1, a), along_rows(OPENED.T, values))


def join_elements(dofs, comp):
    rows = lax.broadcasted_iota(jnp.int32, (8, LANES), 0)
    for axis, step in ((0, 2), (1, 1), (2, 4)):
        if comp == axis:
            continue
        upper = (rows // step) % 2 == 1
        sizes = [3 if comp == other else 4 for other in range(3)]
        sizes[axis] = 1
        for a in range(sizes[0]):
            for b in range(sizes[1]):
                for c in range(sizes[2]):
                    high = [a, b, c]
                    high[axis] = 3
                    to = pl.ds(row_of(comp, a, b, c), 8)
                    moved = pltpu.roll(dofs[pl.ds(row_of(comp, *high), 8), :], step, 0)
                    dofs[to, :] = dofs[to, :] + jnp.where(upper, moved, 0.0)


def scatter_own(vec, dofs):
    for comp in range(3):
        for x, i, a in places(comp, 0):
            for y, j, b in places(comp, 1):
                if x == 6 or y == 6:
                    continue
                for k in range(2):
                    count = 4 if comp != 2 and k == 0 else 3
                    at = row_of(comp, a, b, 0, element(i, j, k))
                    dofs[pl.ds(at, count, 8), :] = vec[comp, x, y, pl.ds(3 * k, count), :]


def scatter_line(dofs, comp, i, a, j, b, source):
    for k in range(2):
        count = 4 if comp != 2 and k == 0 else 3
        at = row_of(comp, a, b, 0, element(i, j, k))
        dofs[pl.ds(at, count, 8), :] = source(pl.ds(3 * k, count))


def scatter_xz_halo(dofs, r_x, r_z, r_e):
    for comp in (1, 2):
        for y, j, b in places(comp, 1):
            if y < 6:
                scatter_line(dofs, comp, 1, 3, j, b, lambda z: r_x[comp - 1, y, z, :])
    for x, i, a in places(0, 0):
        for j in range(2):
            count = 4 - j
            at = row_of(0, a, 0, 3, element(i, j, 1))
            dofs[pl.ds(at, count, 32), :] = r_z[0, x, pl.ds(3 * j, count), :]
    for x, i, a in places(1, 0):
        if x < 6:
            for j in range(2):
                at = row_of(1, a, 0, 3, element(i, j, 1))
                dofs[pl.ds(at, 3, 32), :] = r_z[1, x, pl.ds(3 * j, 3), :]
    for j in range(2):
        at = row_of(1, 3, 0, 3, element(1, j, 1))
        dofs[pl.ds(at, 3, 32), :] = r_e[1, pl.ds(3 * j, 3), :]


def scatter_y_halo(dofs, r_y, r_e):
    for comp in (0, 2):
        for x, i, a in places(comp, 0):
            if x < 6:
                scatter_line(dofs, comp, i, a, 1, 3, lambda z: r_y[comp // 2, x, z, :])
    scatter_line(dofs, 2, 1, 3, 1, 3, lambda z: r_e[2, z, :])
    for i in range(2):
        at = row_of(0, 0, 3, 3, element(i, 1, 1))
        dofs[pl.ds(at, 3, 128), :] = r_e[0, pl.ds(3 * i, 3), :]


def runs(comp, axis, fixed):
    local = [None if g is None else owners(comp, n)[g][1:] for n, g in enumerate(fixed)]
    result = []
    for half in range(2):
        count = 3 + half * (comp != axis)
        at = [(half, 0) if entry is None else entry for entry in local]
        (i, a), (j, b), (k, c) = at
        row = row_of(comp, a, b, c, element(i, j, k))
        result.append((pl.ds(3 * half, count), pl.ds(row, count, 8 * STRIDE[comp][axis])))
    return result


def owned(comp, axis):
    return range(6 if comp == axis else 7)


def to_grid(dofs, comp, out, line):
    other = 3 - line
    for x in owned(comp, 0):
        for q in owned(comp, other):
            fixed = [x, None, None]
            fixed[other] = q
            for grid, rows in runs(comp, line, fixed):
                out[x, q, grid, :] = dofs[rows, :]


def pack_face(dofs, comp, axis, line, pack):
    third = 3 - axis - line
    for side in range(2):
        for p in owned(comp, third):
            fixed = [None] * 3
            fixed[axis] = 6 * side
            fixed[third] = p
            for grid, rows in runs(comp, line, fixed):
                pack[side, p, grid, :] = dofs[rows, :]


def add_face(dofs, comp, axis, line, given):
    third = 3 - axis - line
    for side in range(2):
        for p in owned(comp, third):
            fixed = [None] * 3
            fixed[axis] = 6 * side
            fixed[third] = p
            for grid, rows in runs(comp, line, fixed):
                dofs[rows, :] = dofs[rows, :] + given[side, p, grid, :]


def edge_runs(comp, n):
    fixed = [None] * 3
    for axis, sign in zip(EDGE_AXES[comp], SIGNS[n]):
        fixed[axis] = 6 * (sign > 0)
    return runs(comp, comp, fixed)


def pack_edges(dofs, comp, edges):
    for n in range(4):
        for grid, rows in edge_runs(comp, n):
            edges[comp, n, grid, :] = dofs[rows, :]


def add_edges(dofs, comp, given):
    for n in range(4):
        for grid, rows in edge_runs(comp, n):
            dofs[rows, :] = dofs[rows, :] + given[comp, n, grid, :]


def kernel(
    sizes,
    vec_hbm,
    flip_hbm,
    rel_hbm,
    con_hbm,
    out_x,
    out_y,
    out_z,
    vec,
    flip,
    rel,
    con,
    flat,
    sign,
    mass,
    curl,
    dofs,
    temp,
    u_x,
    u_y,
    c_x,
    c_y,
    c_z,
    s_z,
    s_e,
    r_x,
    r_y,
    r_z,
    r_e,
    t_x,
    t_z,
    p_xy,
    p_xz,
    p_yx,
    p_yz,
    p_zx,
    p_zy,
    p_e,
    f_xy,
    f_xz,
    f_yx,
    f_yz,
    f_zx,
    f_zy,
    f_e,
    load_sem,
    send_sem,
    recv_sem,
):
    me = [lax.axis_index(axis) for axis in AXES]

    def neighbour(*steps):
        return tuple(lax.rem(me[n] + steps[n] + sizes[n], sizes[n]) for n in range(3))

    loads = [
        pltpu.make_async_copy(source, target, load_sem.at[n])
        for n, (source, target) in enumerate(
            ((vec_hbm, vec), (flip_hbm, flip), (rel_hbm, rel), (con_hbm, con))
        )
    ]
    for copy in loads:
        copy.start()

    barrier = pltpu.get_barrier_semaphore()
    around = []
    for axis in range(3):
        for step in (-1, 1):
            around.append([step * (axis == n) for n in range(3)])
    for pair in EDGE_AXES:
        for first, second in SIGNS:
            around.append([first * (n == pair[0]) + second * (n == pair[1]) for n in range(3)])
    for steps in around:
        pl.semaphore_signal(barrier, inc=1, device_id=neighbour(*steps), device_id_type=MESH)

    copies = []

    def send(source, target, *steps):
        n = len(copies)
        copy = pltpu.make_async_remote_copy(
            src_ref=source,
            dst_ref=target,
            send_sem=send_sem.at[n],
            recv_sem=recv_sem.at[n],
            device_id=neighbour(*steps),
            device_id_type=MESH,
        )
        copy.start()
        copies.append(copy)
        return copy

    def send_faces(axis, pack, target):
        faces = []
        for side in range(2):
            steps = [(2 * side - 1) * (axis == n) for n in range(3)]
            faces.append(send(pack.at[side], target.at[1 - side], *steps))
        return faces

    def send_edges(comp):
        sent = []
        for n, pair in enumerate(SIGNS):
            steps = [0, 0, 0]
            for axis, step in zip(EDGE_AXES[comp], pair):
                steps[axis] = step
            sent.append(send(p_e.at[comp, n], f_e.at[comp, 3 - n], *steps))
        return sent

    def receive(arriving):
        for copy in arriving:
            copy.wait_recv()

    loads[0].wait()
    for comp in range(2):
        for x in range(6):
            for y in range(6):
                s_z[comp, x, pl.ds(y, 1), :] = vec[comp, x, y, pl.ds(0, 1), :]
    for n in range(6):
        s_e[0, pl.ds(n, 1), :] = vec[0, n, 0, pl.ds(0, 1), :]
        s_e[1, pl.ds(n, 1), :] = vec[1, 0, n, pl.ds(0, 1), :]
    pl.semaphore_wait(barrier, len(around))
    y_halo = [
        send(vec.at[0, :, 0], r_y.at[0], 0, -1, 0),
        send(vec.at[2, :, 0], r_y.at[1], 0, -1, 0),
    ]
    xz_halo = [
        send(vec.at[pl.ds(1, 2), 0], r_x, -1, 0, 0),
        send(s_z, r_z, 0, 0, -1),
        send(s_e.at[1], r_e.at[1], -1, 0, -1),
    ]
    y_halo += [
        send(s_e.at[0], r_e.at[0], 0, -1, -1),
        send(vec.at[2, 0, 0], r_e.at[2], -1, -1, 0),
    ]

    scatter_own(vec, dofs)
    for copy in loads[1:]:
        copy.wait()
    prepare(flip, rel, con, flat, sign, mass, curl)
    receive(xz_halo)
    scatter_xz_halo(dofs, r_x, r_z, r_e)
    forward_y(dofs, sign, temp, u_y, c_x, c_z)

    @pl.loop(0, 3)
    def _(b):
        start_x(dofs, sign, t_x, b)
        start_z(dofs, sign, t_z, b)

    receive(y_halo)
    scatter_y_halo(dofs, r_y, r_e)
    start_x(dofs, sign, t_x, 3)
    start_z(dofs, sign, t_z, 3)
    forward_x(t_x, curl, u_x, c_y, c_z)
    turn_z(t_z, mass, curl, c_x, c_y)
    finish_z(dofs, sign, t_z)
    join_elements(dofs, 2)
    pack_face(dofs, 2, 1, 2, p_yz)
    faces_yz = send_faces(1, p_yz, f_yz)
    pack_edges(dofs, 2, p_e)
    edges_z = send_edges(2)
    pack_face(dofs, 2, 0, 1, p_xz)
    faces_xz = send_faces(0, p_xz, f_xz)

    backward_x(dofs, sign, mass, t_x, u_x, c_y, c_z)
    join_elements(dofs, 0)
    pack_face(dofs, 0, 1, 2, p_yx)
    faces_yx = send_faces(1, p_yx, f_yx)
    pack_edges(dofs, 0, p_e)
    edges_x = send_edges(0)
    pack_face(dofs, 0, 2, 1, p_zx)
    faces_zx = send_faces(2, p_zx, f_zx)

    backward_y(dofs, sign, mass, temp, u_y, c_x, c_z)
    join_elements(dofs, 1)
    pack_face(dofs, 1, 0, 2, p_xy)
    faces_xy = send_faces(0, p_xy, f_xy)
    pack_edges(dofs, 1, p_e)
    edges_y = send_edges(1)
    pack_face(dofs, 1, 2, 1, p_zy)
    faces_zy = send_faces(2, p_zy, f_zy)

    receive(faces_zx)
    add_face(dofs, 0, 2, 1, f_zx)
    to_grid(dofs, 0, out_x, 2)
    receive(faces_yz + edges_z)
    add_face(dofs, 2, 1, 2, f_yz)
    add_edges(dofs, 2, f_e)
    to_grid(dofs, 2, out_z, 1)
    receive(faces_xz)
    for side in range(2):
        out_z[6 * side] = out_z[6 * side] + f_xz[side]
    receive(faces_zy + edges_y)
    add_face(dofs, 1, 2, 1, f_zy)
    add_edges(dofs, 1, f_e)
    to_grid(dofs, 1, out_y, 2)
    receive(faces_xy)
    for side in range(2):
        out_y[6 * side] = out_y[6 * side] + f_xy[side]
    receive(edges_x)
    for n, pair in enumerate(SIGNS):
        y, z = 6 * (pair[0] > 0), 6 * (pair[1] > 0)
        for x in range(6):
            at = pl.ds(z, 1)
            out_x[x, y, at, :] = out_x[x, y, at, :] + f_e[0, n, pl.ds(x, 1), :]
    receive(faces_yx)
    for side in range(2):
        for x in range(6):
            out_x[x, 6 * side] = out_x[x, 6 * side] + f_yx[side, x]
    for copy in copies:
        copy.wait_send()


def put_out(in_x, in_y, in_z, out_x, out_y, out_z, sem):
    pairs = ((in_x, out_x), (in_y, out_y), (in_z, out_z))
    copies = [pltpu.make_async_copy(*pair, sem.at[n]) for n, pair in enumerate(pairs)]
    for copy in copies:
        copy.start()
    for copy in copies:
        copy.wait()


def on_device(sizes, vectors, orient_flip, reluctivity, conductivity):
    f32 = jnp.float32
    regs = lambda n: pltpu.VMEM((n, 8, LANES), f32)
    grid = ((6, 7, 7, LANES), (7, 6, 7, LANES), (7, 6, 7, LANES))
    faces = [
        pltpu.VMEM(shape, f32)
        for shape in (
            (2, 6, 7, LANES),
            (2, 6, 7, LANES),
            (2, 6, 7, LANES),
            (2, 7, 6, LANES),
            (2, 6, 7, LANES),
            (2, 7, 6, LANES),
            (3, 4, 6, LANES),
        )
    ]
    results = pl.pallas_call(
        lambda *refs: kernel(sizes, *refs),
        out_shape=[pltpu.VMEM(shape, f32) for shape in grid],
        in_specs=[pl.BlockSpec(memory_space=pl.ANY)] * 4,
        out_specs=[pl.BlockSpec(memory_space=pltpu.VMEM)] * 3,
        scratch_shapes=[
            pltpu.VMEM((3, 6, 6, 6, LANES), f32),
            pltpu.VMEM(orient_flip.shape, jnp.int32),
            pltpu.VMEM(reluctivity.shape, f32),
            pltpu.VMEM(conductivity.shape, f32),
            pltpu.VMEM((8, 512), f32),
            regs(DOFS),
            regs(QPTS),
            regs(QPTS),
            pltpu.VMEM((8 * DOFS, LANES), f32),
            regs(QPTS),
            regs(QPTS),
            regs(QPTS),
            regs(QPTS),
            regs(QPTS),
            regs(QPTS),
            pltpu.VMEM((2, 6, 6, LANES), f32),
            pltpu.VMEM((2, 6, LANES), f32),
            pltpu.VMEM((2, 6, 6, LANES), f32),
            pltpu.VMEM((2, 6, 6, LANES), f32),
            pltpu.VMEM((2, 6, 6, LANES), f32),
            pltpu.VMEM((3, 6, LANES), f32),
            regs(QPTS),
            regs(QPTS),
            *faces,
            *faces,
            pltpu.SemaphoreType.DMA((4,)),
            pltpu.SemaphoreType.DMA((31,)),
            pltpu.SemaphoreType.DMA((31,)),
        ],
        compiler_params=pltpu.CompilerParams(collective_id=0, has_side_effects=True),
        name="curlcurl",
    )(vectors, orient_flip, reluctivity, conductivity)
    results = [pltpu.with_memory_space_constraint(result, pltpu.VMEM) for result in results]
    out_x, out_y, out_z = pl.pallas_call(
        put_out,
        out_shape=[jax.ShapeDtypeStruct(shape, f32) for shape in grid],
        in_specs=[pl.BlockSpec(memory_space=pltpu.VMEM)] * 3,
        out_specs=[pl.BlockSpec(memory_space=pl.ANY)] * 3,
        scratch_shapes=[pltpu.SemaphoreType.DMA((3,))],
        name="putout",
    )(*results)
    return (out_x, out_y, jnp.swapaxes(out_z, 1, 2))


def solution(mesh):
    sizes = tuple(mesh.shape[axis] for axis in AXES)
    return jax.shard_map(
        lambda *args: on_device(sizes, *args),
        mesh=mesh,
        in_specs=(
            P(None, "gx", "gy", "gz", None),
            P("gx", "gy", "gz"),
            P("gx", "gy", "gz"),
            P("gx", "gy", "gz"),
        ),
        out_specs=(P("gx", "gy", "gz", None), P("gx", "gy", "gz", None), P("gx", "gy", "gz", None)),
        check_vma=False,
    )
```

time: 33 us -> 27.2 us (0.82)
  the two profiles are of different devices: /device:TPU:24 before, /device:TPU:1 now
where the time goes in v1:
time: 27.2 us; the launch traced here: 26.7 us
  Pallas kernels  26.1 us (96%)
  between operations  0.64 us (2%)
    pallas_call x1, Pallas kernels, on_device(): pl.pallas_call(lambda *refs: kernel(sizes, *refs), out_shape=[pltpu.VMEM(...  25.3 us
    pallas_call x1, Pallas kernels, on_device(): pl.pallas_call(put_out, out_shape=[jax.ShapeDtypeStruct(shape, f32) for s...  0.79 us

profile of v1, /device:TPU:1, one launch (start us, length us, event | category | flops | bytes accessed | tf_op | source)
XLA Modules:
  0.0 26.7 jit_solution(17669488946222623450)
XLA Ops:
  0.6 25.3 %curlcurl.1 = (f32[6,7,7,128]{3,2,1,0:T(8,128)S(1)}, f32[7,6,7,128]{3,2,1,0:T(8,128)S(1)}, f32[7,6,7,128]{3,2,1,0:T(8,128)S(1)}) custom-call(f32[3,6,6,6,128]{4,3,2,1,0:T(8,128)} %refs_0_.1, s32[2,2,288]{2,1,0:T(2,128)} %refs_1_.1, f32[2,2,128]{2,1,0:T(2,128)} %refs_2_.1, f32[2,2,128]{2,1,0:T(2,128)} %refs_3_.1), custom_call_target="tpu_custom_call" | custom-call | tf_op jit(solution)/shard_map/curlcurl/pallas_call | solution.py:639
  25.9 0.8 %putout.1 = (f32[6,7,7,128]{3,2,1,0:T(8,128)}, f32[7,6,7,128]{3,2,1,0:T(8,128)}, f32[7,6,7,128]{3,2,1,0:T(8,128)}) custom-call(f32[6,7,7,128]{3,2,1,0:T(8,128)S(1)} %get-tuple-element.9.in_x, f32[7,6,7,128]{3,2,1,0:T(8,128)S(1)} %get-tuple-element.10.in_y, f32[7,6,7,128]{3,2,1,0:T(8,128)S(1)} %get-tuple-element.11.in_z), custom_call_target="tpu_custom_call" | custom-call | tf_op jit(solution)/shard_map/putout/pallas_call | solution.py:678

commit v2 on v1

--- a/solution.py
+++ b/solution.py
@@ -327,7 +327,6 @@
         for x, i, a in places(comp, 0):
             if x < 6:
                 scatter_line(dofs, comp, i, a, 1, 3, lambda z: r_y[comp // 2, x, z, :])
-    scatter_line(dofs, 2, 1, 3, 1, 3, lambda z: r_e[2, z, :])
     for i in range(2):
         at = row_of(0, 0, 3, 3, element(i, 1, 1))
         dofs[pl.ds(at, 3, 128), :] = r_e[0, pl.ds(3 * i, 3), :]
@@ -465,14 +464,8 @@
         copy.start()
 
     barrier = pltpu.get_barrier_semaphore()
-    around = []
-    for axis in range(3):
-        for step in (-1, 1):
-            around.append([step * (axis == n) for n in range(3)])
-    for pair in EDGE_AXES:
-        for first, second in SIGNS:
-            around.append([first * (n == pair[0]) + second * (n == pair[1]) for n in range(3)])
-    for steps in around:
+    upper = ((0, 1, 0), (1, 1, 0), (0, 1, 1), (1, 0, 0), (1, 0, 1), (0, 0, 1))
+    for steps in upper:
         pl.semaphore_signal(barrier, inc=1, device_id=neighbour(*steps), device_id_type=MESH)
 
     copies = []
@@ -519,19 +512,17 @@
     for n in range(6):
         s_e[0, pl.ds(n, 1), :] = vec[0, n, 0, pl.ds(0, 1), :]
         s_e[1, pl.ds(n, 1), :] = vec[1, 0, n, pl.ds(0, 1), :]
-    pl.semaphore_wait(barrier, len(around))
+    pl.semaphore_wait(barrier, len(upper))
+    xy_halo = [send(vec.at[2, 0, 0], r_e.at[2], -1, -1, 0)]
     y_halo = [
+        send(s_e.at[0], r_e.at[0], 0, -1, -1),
         send(vec.at[0, :, 0], r_y.at[0], 0, -1, 0),
         send(vec.at[2, :, 0], r_y.at[1], 0, -1, 0),
     ]
     xz_halo = [
+        send(s_e.at[1], r_e.at[1], -1, 0, -1),
         send(vec.at[pl.ds(1, 2), 0], r_x, -1, 0, 0),
         send(s_z, r_z, 0, 0, -1),
-        send(s_e.at[1], r_e.at[1], -1, 0, -1),
-    ]
-    y_halo += [
-        send(s_e.at[0], r_e.at[0], 0, -1, -1),
-        send(vec.at[2, 0, 0], r_e.at[2], -1, -1, 0),
     ]
 
     scatter_own(vec, dofs)
@@ -550,33 +541,35 @@
     receive(y_halo)
     scatter_y_halo(dofs, r_y, r_e)
     start_x(dofs, sign, t_x, 3)
+    forward_x(t_x, curl, u_x, c_y, c_z)
+    receive(xy_halo)
+    scatter_line(dofs, 2, 1, 3, 1, 3, lambda z: r_e[2, z, :])
     start_z(dofs, sign, t_z, 3)
-    forward_x(t_x, curl, u_x, c_y, c_z)
     turn_z(t_z, mass, curl, c_x, c_y)
     finish_z(dofs, sign, t_z)
     join_elements(dofs, 2)
+    pack_edges(dofs, 2, p_e)
+    edges_z = send_edges(2)
     pack_face(dofs, 2, 1, 2, p_yz)
     faces_yz = send_faces(1, p_yz, f_yz)
-    pack_edges(dofs, 2, p_e)
-    edges_z = send_edges(2)
     pack_face(dofs, 2, 0, 1, p_xz)
     faces_xz = send_faces(0, p_xz, f_xz)
 
     backward_x(dofs, sign, mass, t_x, u_x, c_y, c_z)
     join_elements(dofs, 0)
+    pack_edges(dofs, 0, p_e)
+    edges_x = send_edges(0)
     pack_face(dofs, 0, 1, 2, p_yx)
     faces_yx = send_faces(1, p_yx, f_yx)
-    pack_edges(dofs, 0, p_e)
-    edges_x = send_edges(0)
     pack_face(dofs, 0, 2, 1, p_zx)
     faces_zx = send_faces(2, p_zx, f_zx)
 
     backward_y(dofs, sign, mass, temp, u_y, c_x, c_z)
     join_elements(dofs, 1)
+    pack_edges(dofs, 1, p_e)
+    edges_y = send_edges(1)
     pack_face(dofs, 1, 0, 2, p_xy)
     faces_xy = send_faces(0, p_xy, f_xy)
-    pack_edges(dofs, 1, p_e)
-    edges_y = send_edges(1)
     pack_face(dofs, 1, 2, 1, p_zy)
     faces_zy = send_faces(2, p_zy, f_zy)
 

time: 27.2 us -> 26.6 us (0.978); the launches traced: 26.7 us -> 26.5 us
  no operation moved by 1% of the time
where the time goes in v2:
time: 26.6 us; the launch traced here: 26.5 us
  Pallas kernels  25.9 us (97%)
  between operations  0.64 us (2%)
    pallas_call x1, Pallas kernels, on_device(): pl.pallas_call(lambda *refs: kernel(sizes, *refs), out_shape=[pltpu.VMEM(...  25.1 us
    pallas_call x1, Pallas kernels, on_device(): pl.pallas_call(put_out, out_shape=[jax.ShapeDtypeStruct(shape, f32) for s...  0.79 us

profile of v2, /device:TPU:1, one launch (start us, length us, event | category | flops | bytes accessed | tf_op | source)
XLA Modules:
  0.0 26.5 jit_solution(6045208302343917960)
XLA Ops:
  0.6 25.1 %curlcurl.1 = (f32[6,7,7,128]{3,2,1,0:T(8,128)S(1)}, f32[7,6,7,128]{3,2,1,0:T(8,128)S(1)}, f32[7,6,7,128]{3,2,1,0:T(8,128)S(1)}) custom-call(f32[3,6,6,6,128]{4,3,2,1,0:T(8,128)} %refs_0_.1, s32[2,2,288]{2,1,0:T(2,128)} %refs_1_.1, f32[2,2,128]{2,1,0:T(2,128)} %refs_2_.1, f32[2,2,128]{2,1,0:T(2,128)} %refs_3_.1), custom_call_target="tpu_custom_call" | custom-call | tf_op jit(solution)/shard_map/curlcurl/pallas_call | solution.py:632
  25.7 0.8 %putout.1 = (f32[6,7,7,128]{3,2,1,0:T(8,128)}, f32[7,6,7,128]{3,2,1,0:T(8,128)}, f32[7,6,7,128]{3,2,1,0:T(8,128)}) custom-call(f32[6,7,7,128]{3,2,1,0:T(8,128)S(1)} %get-tuple-element.9.in_x, f32[7,6,7,128]{3,2,1,0:T(8,128)S(1)} %get-tuple-element.10.in_y, f32[7,6,7,128]{3,2,1,0:T(8,128)S(1)} %get-tuple-element.11.in_z), custom_call_target="tpu_custom_call" | custom-call | tf_op jit(solution)/shard_map/putout/pallas_call | solution.py:671

commit v3 on v2

--- a/solution.py
+++ b/solution.py
@@ -177,12 +177,12 @@
 
 
 def forward_y(dofs, sign, temp, u_y, c_x, c_z):
-    @pl.loop(0, 4)
+    @pl.loop(0, 4, unroll=2)
     def _(a):
         values = along_rows(OPENED, load_plane(dofs, sign, rows_fixed_a(1, a)))
         put(temp, lambda y, z: quad(a, y, z), along_columns(CLOSED, values))
 
-    @pl.loop(0, 4)
+    @pl.loop(0, 4, unroll=2)
     def _(y):
         at = lambda x, z: quad(x, y, z)
         u = along_rows(CLOSED, planes(temp, at))
@@ -202,7 +202,7 @@
 
 
 def forward_x(temp, curl, u_x, c_y, c_z):
-    @pl.loop(0, 4)
+    @pl.loop(0, 4, unroll=2)
     def _(x):
         at = lambda y, z: quad(x, y, z)
         u = along_rows(CLOSED, planes(temp, at))
@@ -213,7 +213,7 @@
 
 
 def turn_z(temp, mass, curl, c_x, c_y):
-    @pl.loop(0, 4)
+    @pl.loop(0, 4, unroll=2)
     def _(z):
         at = lambda x, y: quad(x, y, z)
         u = along_columns(CLOSED, planes(temp, at))
@@ -229,14 +229,14 @@
 
 
 def finish_z(dofs, sign, temp):
-    @pl.loop(0, 4)
+    @pl.loop(0, 4, unroll=2)
     def _(b):
         values = along_rows(CLOSED.T, planes(temp, lambda x, z: quad(x, b, z)))
         store_plane(dofs, sign, rows_fixed_b(2, b), along_columns(OPENED.T, values))
 
 
 def backward_x(dofs, sign, mass, temp, u_x, c_y, c_z):
-    @pl.loop(0, 4)
+    @pl.loop(0, 4, unroll=2)
     def _(x):
         at = lambda y, z: quad(x, y, z)
         v = times(planes(mass, at), planes(u_x, at))
@@ -244,14 +244,14 @@
         v = minus(v, along_rows(DERIV.T, planes(c_z, at), -1))
         put(temp, at, along_rows(CLOSED.T, v))
 
-    @pl.loop(0, 4)
+    @pl.loop(0, 4, unroll=2)
     def _(b):
         values = along_columns(CLOSED.T, planes(temp, lambda x, z: quad(x, b, z)))
         store_plane(dofs, sign, rows_fixed_b(0, b), along_rows(OPENED.T, values))
 
 
 def backward_y(dofs, sign, mass, temp, u_y, c_x, c_z):
-    @pl.loop(0, 4)
+    @pl.loop(0, 4, unroll=2)
     def _(y):
         at = lambda x, z: quad(x, y, z)
         v = times(planes(mass, at), planes(u_y, at))
@@ -259,7 +259,7 @@
         v = minus(v, along_columns(DERIV.T, planes(c_x, at), -1))
         put(temp, at, along_rows(CLOSED.T, v))
 
-    @pl.loop(0, 4)
+    @pl.loop(0, 4, unroll=2)
     def _(a):
         values = along_columns(CLOSED.T, planes(temp, lambda y, z: quad(a, y, z)))
         store_plane(dofs, sign, rows_fixed_a(1, a), along_rows(OPENED.T, values))
@@ -302,7 +302,7 @@
         dofs[pl.ds(at, count, 8), :] = source(pl.ds(3 * k, count))
 
 
-def scatter_xz_halo(dofs, r_x, r_z, r_e):
+def scatter_xz_halo(dofs, r_x, r_z):
     for comp in (1, 2):
         for y, j, b in places(comp, 1):
             if y < 6:
@@ -317,6 +317,9 @@
             for j in range(2):
                 at = row_of(1, a, 0, 3, element(i, j, 1))
                 dofs[pl.ds(at, 3, 32), :] = r_z[1, x, pl.ds(3 * j, 3), :]
+
+
+def scatter_xz_edge(dofs, r_e):
     for j in range(2):
         at = row_of(1, 3, 0, 3, element(1, j, 1))
         dofs[pl.ds(at, 3, 32), :] = r_e[1, pl.ds(3 * j, 3), :]
@@ -529,15 +532,17 @@
     for copy in loads[1:]:
         copy.wait()
     prepare(flip, rel, con, flat, sign, mass, curl)
-    receive(xz_halo)
-    scatter_xz_halo(dofs, r_x, r_z, r_e)
-    forward_y(dofs, sign, temp, u_y, c_x, c_z)
-
-    @pl.loop(0, 3)
+    receive(xz_halo[1:])
+    scatter_xz_halo(dofs, r_x, r_z)
+
+    @pl.loop(0, 3, unroll=1)
     def _(b):
         start_x(dofs, sign, t_x, b)
         start_z(dofs, sign, t_z, b)
 
+    receive(xz_halo[:1])
+    scatter_xz_edge(dofs, r_e)
+    forward_y(dofs, sign, temp, u_y, c_x, c_z)
     receive(y_halo)
     scatter_y_halo(dofs, r_y, r_e)
     start_x(dofs, sign, t_x, 3)

time: 26.6 us -> 26.2 us (0.985)
  Pallas kernels: 25.9 us -> 25.4 us
    pallas_call x1, Pallas kernels: 25.1 us -> 24.6 us  [on_device(): pl.pallas_call(lambda *refs: kernel(sizes, *refs), out_shape=[pltpu.VMEM(...]
where the time goes in v3:
time: 26.2 us; the launch traced here: 26.1 us
  Pallas kernels  25.4 us (97%)
  between operations  0.64 us (2%)
    pallas_call x1, Pallas kernels, on_device(): pl.pallas_call(lambda *refs: kernel(sizes, *refs), out_shape=[pltpu.VMEM(...  24.6 us
    pallas_call x1, Pallas kernels, on_device(): pl.pallas_call(put_out, out_shape=[jax.ShapeDtypeStruct(shape, f32) for s...  0.79 us

profile of v3, /device:TPU:1, one launch (start us, length us, event | category | flops | bytes accessed | tf_op | source)
XLA Modules:
  0.0 26.1 jit_solution(15251470093936023480)
XLA Ops:
  0.6 24.6 %curlcurl.1 = (f32[6,7,7,128]{3,2,1,0:T(8,128)S(1)}, f32[7,6,7,128]{3,2,1,0:T(8,128)S(1)}, f32[7,6,7,128]{3,2,1,0:T(8,128)S(1)}) custom-call(f32[3,6,6,6,128]{4,3,2,1,0:T(8,128)} %refs_0_.1, s32[2,2,288]{2,1,0:T(2,128)} %refs_1_.1, f32[2,2,128]{2,1,0:T(2,128)} %refs_2_.1, f32[2,2,128]{2,1,0:T(2,128)} %refs_3_.1), custom_call_target="tpu_custom_call" | custom-call | tf_op jit(solution)/shard_map/curlcurl/pallas_call | solution.py:637
  25.3 0.8 %putout.1 = (f32[6,7,7,128]{3,2,1,0:T(8,128)}, f32[7,6,7,128]{3,2,1,0:T(8,128)}, f32[7,6,7,128]{3,2,1,0:T(8,128)}) custom-call(f32[6,7,7,128]{3,2,1,0:T(8,128)S(1)} %get-tuple-element.9.in_x, f32[7,6,7,128]{3,2,1,0:T(8,128)S(1)} %get-tuple-element.10.in_y, f32[7,6,7,128]{3,2,1,0:T(8,128)S(1)} %get-tuple-element.11.in_z), custom_call_target="tpu_custom_call" | custom-call | tf_op jit(solution)/shard_map/putout/pallas_call | solution.py:676

commit v4 on v3

--- a/solution.py
+++ b/solution.py
@@ -48,15 +48,16 @@
 
 CLOSED, SLOPES, OPENED, WEIGHT = basis_tables()
 DERIV = SLOPES @ np.linalg.inv(CLOSED)
-
-
-def apply(table, given, parity):
+OUTER, INNER = (0,), (1,)
+
+
+def apply(table, given, parity, pairs=None):
     rows, columns = table.shape
     half = columns // 2
     sums = [given[c] + given[columns - 1 - c] for c in range(half)]
     diffs = [given[c] - given[columns - 1 - c] for c in range(half)]
     result = [None] * rows
-    for q in range((rows + 1) // 2):
+    for q in pairs or range((rows + 1) // 2):
         even = None
         for c in range(half):
             term = sums[c] * float((table[q, c] + table[q, columns - 1 - c]) / 2)
@@ -75,13 +76,15 @@
     return result
 
 
-def along_rows(table, plane, parity=1):
-    columns = [apply(table, [row[c] for row in plane], parity) for c in range(len(plane[0]))]
+def along_rows(table, plane, parity=1, pairs=None):
+    columns = [
+        apply(table, [row[c] for row in plane], parity, pairs) for c in range(len(plane[0]))
+    ]
     return [[column[q] for column in columns] for q in range(table.shape[0])]
 
 
-def along_columns(table, plane, parity=1):
-    return [apply(table, row, parity) for row in plane]
+def along_columns(table, plane, parity=1, pairs=None):
+    return [apply(table, row, parity, pairs) for row in plane]
 
 
 def combine(op, *planes):
@@ -153,7 +156,8 @@
 def put(ref, at, plane):
     for p, row in enumerate(plane):
         for q, value in enumerate(row):
-            ref[at(p, q)] = value
+            if value is not None:
+                ref[at(p, q)] = value
 
 
 def load_plane(dofs, sign, rows):
@@ -177,12 +181,12 @@
 
 
 def forward_y(dofs, sign, temp, u_y, c_x, c_z):
-    @pl.loop(0, 4, unroll=2)
+    @pl.loop(0, 4, unroll=True)
     def _(a):
         values = along_rows(OPENED, load_plane(dofs, sign, rows_fixed_a(1, a)))
         put(temp, lambda y, z: quad(a, y, z), along_columns(CLOSED, values))
 
-    @pl.loop(0, 4, unroll=2)
+    @pl.loop(0, 4, unroll=True)
     def _(y):
         at = lambda x, z: quad(x, y, z)
         u = along_rows(CLOSED, planes(temp, at))
@@ -202,7 +206,7 @@
 
 
 def forward_x(temp, curl, u_x, c_y, c_z):
-    @pl.loop(0, 4, unroll=2)
+    @pl.loop(0, 4, unroll=True)
     def _(x):
         at = lambda y, z: quad(x, y, z)
         u = along_rows(CLOSED, planes(temp, at))
@@ -212,8 +216,8 @@
         put(c_y, at, along_columns(DERIV, u, -1))
 
 
-def turn_z(temp, mass, curl, c_x, c_y):
-    @pl.loop(0, 4, unroll=2)
+def turn_z(temp, kept, mass, curl, c_x, c_y):
+    @pl.loop(0, 4, unroll=True)
     def _(z):
         at = lambda x, y: quad(x, y, z)
         u = along_columns(CLOSED, planes(temp, at))
@@ -225,33 +229,51 @@
         v = times(planes(mass, at), u)
         v = plus(v, along_columns(DERIV.T, w_x, -1))
         v = minus(v, along_rows(DERIV.T, w_y, -1))
-        put(temp, at, along_columns(CLOSED.T, v))
-
-
-def finish_z(dofs, sign, temp):
-    @pl.loop(0, 4, unroll=2)
+        put(kept, at, v)
+        put(temp, at, along_columns(CLOSED.T, v, 1, OUTER))
+
+
+def inner_z(temp, kept):
+    @pl.loop(0, 4, unroll=True)
+    def _(z):
+        at = lambda x, y: quad(x, y, z)
+        put(temp, at, along_columns(CLOSED.T, planes(kept, at), 1, INNER))
+
+
+def finish_z(dofs, sign, temp, first, last, step):
+    @pl.loop(first, last, step=step, unroll=True)
     def _(b):
         values = along_rows(CLOSED.T, planes(temp, lambda x, z: quad(x, b, z)))
         store_plane(dofs, sign, rows_fixed_b(2, b), along_columns(OPENED.T, values))
 
 
-def backward_x(dofs, sign, mass, temp, u_x, c_y, c_z):
-    @pl.loop(0, 4, unroll=2)
+def backward_x(mass, temp, kept, u_x, c_y, c_z):
+    @pl.loop(0, 4, unroll=True)
     def _(x):
         at = lambda y, z: quad(x, y, z)
         v = times(planes(mass, at), planes(u_x, at))
         v = plus(v, along_columns(DERIV.T, planes(c_y, at), -1))
         v = minus(v, along_rows(DERIV.T, planes(c_z, at), -1))
-        put(temp, at, along_rows(CLOSED.T, v))
-
-    @pl.loop(0, 4, unroll=2)
+        put(kept, at, v)
+        put(temp, at, along_rows(CLOSED.T, v, 1, OUTER))
+
+
+def inner_x(temp, kept):
+    @pl.loop(0, 4, unroll=True)
+    def _(x):
+        at = lambda y, z: quad(x, y, z)
+        put(temp, at, along_rows(CLOSED.T, planes(kept, at), 1, INNER))
+
+
+def finish_x(dofs, sign, temp, first, last, step):
+    @pl.loop(first, last, step=step, unroll=True)
     def _(b):
         values = along_columns(CLOSED.T, planes(temp, lambda x, z: quad(x, b, z)))
         store_plane(dofs, sign, rows_fixed_b(0, b), along_rows(OPENED.T, values))
 
 
 def backward_y(dofs, sign, mass, temp, u_y, c_x, c_z):
-    @pl.loop(0, 4, unroll=2)
+    @pl.loop(0, 4, unroll=True)
     def _(y):
         at = lambda x, z: quad(x, y, z)
         v = times(planes(mass, at), planes(u_y, at))
@@ -259,23 +281,25 @@
         v = minus(v, along_columns(DERIV.T, planes(c_x, at), -1))
         put(temp, at, along_rows(CLOSED.T, v))
 
-    @pl.loop(0, 4, unroll=2)
+    @pl.loop(0, 4, unroll=True)
     def _(a):
         values = along_columns(CLOSED.T, planes(temp, lambda y, z: quad(a, y, z)))
         store_plane(dofs, sign, rows_fixed_a(1, a), along_rows(OPENED.T, values))
 
 
-def join_elements(dofs, comp):
+def join_elements(dofs, comp, axes=(0, 1, 2), only_b=None):
     rows = lax.broadcasted_iota(jnp.int32, (8, LANES), 0)
     for axis, step in ((0, 2), (1, 1), (2, 4)):
-        if comp == axis:
+        if comp == axis or axis not in axes:
             continue
         upper = (rows // step) % 2 == 1
-        sizes = [3 if comp == other else 4 for other in range(3)]
-        sizes[axis] = 1
-        for a in range(sizes[0]):
-            for b in range(sizes[1]):
-                for c in range(sizes[2]):
+        sizes = [range(3 if comp == other else 4) for other in range(3)]
+        sizes[axis] = range(1)
+        if only_b:
+            sizes[1] = only_b
+        for a in sizes[0]:
+            for b in sizes[1]:
+                for c in sizes[2]:
                     high = [a, b, c]
                     high[axis] = 3
                     to = pl.ds(row_of(comp, a, b, c), 8)
@@ -434,6 +458,8 @@
     r_e,
     t_x,
     t_z,
+    v_x,
+    v_z,
     p_xy,
     p_xz,
     p_yx,
@@ -550,24 +576,21 @@
     receive(xy_halo)
     scatter_line(dofs, 2, 1, 3, 1, 3, lambda z: r_e[2, z, :])
     start_z(dofs, sign, t_z, 3)
-    turn_z(t_z, mass, curl, c_x, c_y)
-    finish_z(dofs, sign, t_z)
-    join_elements(dofs, 2)
+    turn_z(t_z, v_z, mass, curl, c_x, c_y)
+    finish_z(dofs, sign, t_z, 0, 4, 3)
+    join_elements(dofs, 2, (0,), (0, 3))
     pack_edges(dofs, 2, p_e)
     edges_z = send_edges(2)
     pack_face(dofs, 2, 1, 2, p_yz)
     faces_yz = send_faces(1, p_yz, f_yz)
-    pack_face(dofs, 2, 0, 1, p_xz)
-    faces_xz = send_faces(0, p_xz, f_xz)
-
-    backward_x(dofs, sign, mass, t_x, u_x, c_y, c_z)
-    join_elements(dofs, 0)
+
+    backward_x(mass, t_x, v_x, u_x, c_y, c_z)
+    finish_x(dofs, sign, t_x, 0, 4, 3)
+    join_elements(dofs, 0, (2,), (0, 3))
     pack_edges(dofs, 0, p_e)
     edges_x = send_edges(0)
     pack_face(dofs, 0, 1, 2, p_yx)
     faces_yx = send_faces(1, p_yx, f_yx)
-    pack_face(dofs, 0, 2, 1, p_zx)
-    faces_zx = send_faces(2, p_zx, f_zx)
 
     backward_y(dofs, sign, mass, temp, u_y, c_x, c_z)
     join_elements(dofs, 1)
@@ -575,9 +598,29 @@
     edges_y = send_edges(1)
     pack_face(dofs, 1, 0, 2, p_xy)
     faces_xy = send_faces(0, p_xy, f_xy)
+
+    inner_z(t_z, v_z)
+    finish_z(dofs, sign, t_z, 1, 3, 1)
+    join_elements(dofs, 2, (0,), (1, 2))
+    join_elements(dofs, 2, (1,))
+    pack_face(dofs, 2, 0, 1, p_xz)
+    faces_xz = send_faces(0, p_xz, f_xz)
     pack_face(dofs, 1, 2, 1, p_zy)
     faces_zy = send_faces(2, p_zy, f_zy)
-
+    inner_x(t_x, v_x)
+    finish_x(dofs, sign, t_x, 1, 3, 1)
+    join_elements(dofs, 0, (2,), (1, 2))
+    join_elements(dofs, 0, (1,))
+    pack_face(dofs, 0, 2, 1, p_zx)
+    faces_zx = send_faces(2, p_zx, f_zx)
+
+    receive(faces_zy + edges_y)
+    add_face(dofs, 1, 2, 1, f_zy)
+    add_edges(dofs, 1, f_e)
+    to_grid(dofs, 1, out_y, 2)
+    receive(faces_xy)
+    for side in range(2):
+        out_y[6 * side] = out_y[6 * side] + f_xy[side]
     receive(faces_zx)
     add_face(dofs, 0, 2, 1, f_zx)
     to_grid(dofs, 0, out_x, 2)
@@ -588,13 +631,6 @@
     receive(faces_xz)
     for side in range(2):
         out_z[6 * side] = out_z[6 * side] + f_xz[side]
-    receive(faces_zy + edges_y)
-    add_face(dofs, 1, 2, 1, f_zy)
-    add_edges(dofs, 1, f_e)
-    to_grid(dofs, 1, out_y, 2)
-    receive(faces_xy)
-    for side in range(2):
-        out_y[6 * side] = out_y[6 * side] + f_xy[side]
     receive(edges_x)
     for n, pair in enumerate(SIGNS):
         y, z = 6 * (pair[0] > 0), 6 * (pair[1] > 0)
@@ -661,8 +697,7 @@
             pltpu.VMEM((2, 6, 6, LANES), f32),
             pltpu.VMEM((2, 6, 6, LANES), f32),
             pltpu.VMEM((3, 6, LANES), f32),
-            regs(QPTS),
-            regs(QPTS),
+            *[regs(QPTS)] * 4,
             *faces,
             *faces,
             pltpu.SemaphoreType.DMA((4,)),

time: 26.2 us -> 25.9 us (0.989)
  Pallas kernels: 25.4 us -> 25 us
    pallas_call x1, Pallas kernels: 24.6 us -> 24.2 us  [on_device(): pl.pallas_call(lambda *refs: kernel(sizes, *refs), out_shape=[pltpu.VMEM(...]
where the time goes in v4:
time: 25.9 us; the launch traced here: 25.7 us
  Pallas kernels  25 us (97%)
  between operations  0.64 us (2%)
    pallas_call x1, Pallas kernels, on_device(): pl.pallas_call(lambda *refs: kernel(sizes, *refs), out_shape=[pltpu.VMEM(...  24.2 us
    pallas_call x1, Pallas kernels, on_device(): pl.pallas_call(put_out, out_shape=[jax.ShapeDtypeStruct(shape, f32) for s...  0.79 us

profile of v4, /device:TPU:1, one launch (start us, length us, event | category | flops | bytes accessed | tf_op | source)
XLA Modules:
  0.0 25.7 jit_solution(7422321960243269309)
XLA Ops:
  0.6 24.2 %curlcurl.1 = (f32[6,7,7,128]{3,2,1,0:T(8,128)S(1)}, f32[7,6,7,128]{3,2,1,0:T(8,128)S(1)}, f32[7,6,7,128]{3,2,1,0:T(8,128)S(1)}) custom-call(f32[3,6,6,6,128]{4,3,2,1,0:T(8,128)} %refs_0_.1, s32[2,2,288]{2,1,0:T(2,128)} %refs_1_.1, f32[2,2,128]{2,1,0:T(2,128)} %refs_2_.1, f32[2,2,128]{2,1,0:T(2,128)} %refs_3_.1), custom_call_target="tpu_custom_call" | custom-call | tf_op jit(solution)/shard_map/curlcurl/pallas_call | solution.py:673
  24.9 0.8 %putout.1 = (f32[6,7,7,128]{3,2,1,0:T(8,128)}, f32[7,6,7,128]{3,2,1,0:T(8,128)}, f32[7,6,7,128]{3,2,1,0:T(8,128)}) custom-call(f32[6,7,7,128]{3,2,1,0:T(8,128)S(1)} %get-tuple-element.9.in_x, f32[7,6,7,128]{3,2,1,0:T(8,128)S(1)} %get-tuple-element.10.in_y, f32[7,6,7,128]{3,2,1,0:T(8,128)S(1)} %get-tuple-element.11.in_z), custom_call_target="tpu_custom_call" | custom-call | tf_op jit(solution)/shard_map/putout/pallas_call | solution.py:711

commit v5 on v4

--- a/solution.py
+++ b/solution.py
@@ -541,6 +541,7 @@
     for n in range(6):
         s_e[0, pl.ds(n, 1), :] = vec[0, n, 0, pl.ds(0, 1), :]
         s_e[1, pl.ds(n, 1), :] = vec[1, 0, n, pl.ds(0, 1), :]
+    scatter_own(vec, dofs)
     pl.semaphore_wait(barrier, len(upper))
     xy_halo = [send(vec.at[2, 0, 0], r_e.at[2], -1, -1, 0)]
     y_halo = [
@@ -554,7 +555,6 @@
         send(s_z, r_z, 0, 0, -1),
     ]
 
-    scatter_own(vec, dofs)
     for copy in loads[1:]:
         copy.wait()
     prepare(flip, rel, con, flat, sign, mass, curl)
@@ -584,6 +584,13 @@
     pack_face(dofs, 2, 1, 2, p_yz)
     faces_yz = send_faces(1, p_yz, f_yz)
 
+    backward_y(dofs, sign, mass, temp, u_y, c_x, c_z)
+    join_elements(dofs, 1)
+    pack_edges(dofs, 1, p_e)
+    edges_y = send_edges(1)
+    pack_face(dofs, 1, 0, 2, p_xy)
+    faces_xy = send_faces(0, p_xy, f_xy)
+
     backward_x(mass, t_x, v_x, u_x, c_y, c_z)
     finish_x(dofs, sign, t_x, 0, 4, 3)
     join_elements(dofs, 0, (2,), (0, 3))
@@ -591,13 +598,6 @@
     edges_x = send_edges(0)
     pack_face(dofs, 0, 1, 2, p_yx)
     faces_yx = send_faces(1, p_yx, f_yx)
-
-    backward_y(dofs, sign, mass, temp, u_y, c_x, c_z)
-    join_elements(dofs, 1)
-    pack_edges(dofs, 1, p_e)
-    edges_y = send_edges(1)
-    pack_face(dofs, 1, 0, 2, p_xy)
-    faces_xy = send_faces(0, p_xy, f_xy)
 
     inner_z(t_z, v_z)
     finish_z(dofs, sign, t_z, 1, 3, 1)

time: 25.9 us -> 25.7 us (level)
  no operation moved by 1% of the time
where the time goes in v5:
time: 25.7 us; the launch traced here: 25.4 us
  Pallas kernels  24.8 us (96%)
  between operations  0.64 us (2%)
    pallas_call x1, Pallas kernels, on_device(): pl.pallas_call(lambda *refs: kernel(sizes, *refs), out_shape=[pltpu.VMEM(...  24 us
    pallas_call x1, Pallas kernels, on_device(): pl.pallas_call(put_out, out_shape=[jax.ShapeDtypeStruct(shape, f32) for s...  0.79 us

profile of v5, /device:TPU:1, one launch (start us, length us, event | category | flops | bytes accessed | tf_op | source)
XLA Modules:
  0.0 25.4 jit_solution(3231539339779059480)
XLA Ops:
  0.6 24.0 %curlcurl.1 = (f32[6,7,7,128]{3,2,1,0:T(8,128)S(1)}, f32[7,6,7,128]{3,2,1,0:T(8,128)S(1)}, f32[7,6,7,128]{3,2,1,0:T(8,128)S(1)}) custom-call(f32[3,6,6,6,128]{4,3,2,1,0:T(8,128)} %refs_0_.1, s32[2,2,288]{2,1,0:T(2,128)} %refs_1_.1, f32[2,2,128]{2,1,0:T(2,128)} %refs_2_.1, f32[2,2,128]{2,1,0:T(2,128)} %refs_3_.1), custom_call_target="tpu_custom_call" | custom-call | tf_op jit(solution)/shard_map/curlcurl/pallas_call | solution.py:673
  24.7 0.8 %putout.1 = (f32[6,7,7,128]{3,2,1,0:T(8,128)}, f32[7,6,7,128]{3,2,1,0:T(8,128)}, f32[7,6,7,128]{3,2,1,0:T(8,128)}) custom-call(f32[6,7,7,128]{3,2,1,0:T(8,128)S(1)} %get-tuple-element.9.in_x, f32[7,6,7,128]{3,2,1,0:T(8,128)S(1)} %get-tuple-element.10.in_y, f32[7,6,7,128]{3,2,1,0:T(8,128)S(1)} %get-tuple-element.11.in_z), custom_call_target="tpu_custom_call" | custom-call | tf_op jit(solution)/shard_map/putout/pallas_call | solution.py:711

commit v6 on v5

--- a/solution.py
+++ b/solution.py
@@ -515,14 +515,14 @@
 
     def send_faces(axis, pack, target):
         faces = []
-        for side in range(2):
+        for side in (1, 0):
             steps = [(2 * side - 1) * (axis == n) for n in range(3)]
             faces.append(send(pack.at[side], target.at[1 - side], *steps))
         return faces
 
     def send_edges(comp):
         sent = []
-        for n, pair in enumerate(SIGNS):
+        for n, pair in reversed(tuple(enumerate(SIGNS))):
             steps = [0, 0, 0]
             for axis, step in zip(EDGE_AXES[comp], pair):
                 steps[axis] = step

time: 25.7 us -> 25.7 us (level)
  no operation moved by 1% of the time
where the time goes in v6:
time: 25.7 us; the launch traced here: 25.4 us
  Pallas kernels  24.8 us (96%)
  between operations  0.64 us (2%)
    pallas_call x1, Pallas kernels, on_device(): pl.pallas_call(lambda *refs: kernel(sizes, *refs), out_shape=[pltpu.VMEM(...  24 us
    pallas_call x1, Pallas kernels, on_device(): pl.pallas_call(put_out, out_shape=[jax.ShapeDtypeStruct(shape, f32) for s...  0.79 us

profile of v6, /device:TPU:1, one launch (start us, length us, event | category | flops | bytes accessed | tf_op | source)
XLA Modules:
  0.0 25.4 jit_solution(12839870864401831736)
XLA Ops:
  0.6 24.0 %curlcurl.1 = (f32[6,7,7,128]{3,2,1,0:T(8,128)S(1)}, f32[7,6,7,128]{3,2,1,0:T(8,128)S(1)}, f32[7,6,7,128]{3,2,1,0:T(8,128)S(1)}) custom-call(f32[3,6,6,6,128]{4,3,2,1,0:T(8,128)} %refs_0_.1, s32[2,2,288]{2,1,0:T(2,128)} %refs_1_.1, f32[2,2,128]{2,1,0:T(2,128)} %refs_2_.1, f32[2,2,128]{2,1,0:T(2,128)} %refs_3_.1), custom_call_target="tpu_custom_call" | custom-call | tf_op jit(solution)/shard_map/curlcurl/pallas_call | solution.py:673
  24.6 0.8 %putout.1 = (f32[6,7,7,128]{3,2,1,0:T(8,128)}, f32[7,6,7,128]{3,2,1,0:T(8,128)}, f32[7,6,7,128]{3,2,1,0:T(8,128)}) custom-call(f32[6,7,7,128]{3,2,1,0:T(8,128)S(1)} %get-tuple-element.9.in_x, f32[7,6,7,128]{3,2,1,0:T(8,128)S(1)} %get-tuple-element.10.in_y, f32[7,6,7,128]{3,2,1,0:T(8,128)S(1)} %get-tuple-element.11.in_z), custom_call_target="tpu_custom_call" | custom-call | tf_op jit(solution)/shard_map/putout/pallas_call | solution.py:711
